TPU v7x, 32 devices: a whole 2x2x4 slice. The times are simulated.
32 devices in a mesh: ctx: 8 (over z, x), head: 4 (over y, core).
Axes of the slice: x: 2, y: 2, z: 4, core: 2. Of those that a mesh axis runs over, the one named last changes fastest.
Arguments:
- activations: bfloat16 [8192, 2048], P('ctx', 'head'), may hold values from -6 to 6
- w_query: bfloat16 [2048, 2048], P('ctx', 'head'), may hold values from -0.125 to 0.125
- w_key: bfloat16 [2048, 2048], P('ctx', 'head'), may hold values from -0.125 to 0.125
- w_value: bfloat16 [2048, 2048], P('ctx', 'head'), may hold values from -0.125 to 0.125
- level_table: float32 [16, 64, 14], P('head'), may hold values from 0.2 to 2
- table_rows: int32 [8192], P('ctx'), may hold values from 0 to 63
- out_grad: bfloat16 [8192, 2048], P('ctx', 'head'), may hold values from -0.059814453 to 0.059814453
Outputs:
- attended: bfloat16 [8192, 2048], P('ctx', 'head')
- grad_query: float32 [2048, 2048], P('ctx', 'head')
- grad_key: float32 [2048, 2048], P('ctx', 'head')
- grad_value: float32 [2048, 2048], P('ctx', 'head')
All inputs are finite; a program needn't handle non-finite values.
Results may differ from a plain program's by a relative error of at most 0.0056.
Values may be sent and summed in bfloat16 or wider, within the bound.
A program may use at most 64 MiB of HBM per device.

v0:
```python
import math
import jax
import jax.numpy as jnp
from jax import lax
from jax.sharding import PartitionSpec as P


def from_partner(block, axis, apart):
    count = lax.axis_size(axis)
    route = []
    for low in range(count):
        high = low | 1 << apart
        if high != low and high < count:
            route += [(low, high), (high, low)]
    return lax.ppermute(block, axis, route)


def level_of(distance, bit_total):
    running = jnp.zeros(distance.shape, jnp.int32)
    for bit_num in range(bit_total):
        running = running + (distance >= 1 << bit_num).astype(jnp.int32)
    return running


def on_device(activations, w_query, w_key, w_value, level_table, table_rows, out_grad):
    features = lax.all_gather(activations, "head", axis=1, tiled=True)
    row_count = features.shape[0]
    column_count = w_query.shape[1]
    heads_here = level_table.shape[0]
    table_size = level_table.shape[1]
    level_count = level_table.shape[2]
    head_width = column_count // heads_here
    inner_bits = row_count.bit_length() - 1
    outer_bits = lax.axis_size("ctx").bit_length() - 1
    my_index = lax.axis_index("ctx")
    scale_factor = 1.0 / math.sqrt(head_width * row_count)
    highest = lax.Precision.HIGHEST
    pieces = (
        lax.all_gather(w_query, "ctx", axis=0, tiled=True),
        lax.all_gather(w_key, "ctx", axis=0, tiled=True),
        lax.all_gather(w_value, "ctx", axis=0, tiled=True),
    )
    feature_cols = features
    projected = tuple(
        (
            jnp.dot(feature_cols, weight_piece, preferred_element_type=jnp.float32)
            for weight_piece in pieces
        )
    )
    queries = projected[0].astype(jnp.bfloat16).reshape(row_count, heads_here, head_width)
    key_proj = projected[1].astype(jnp.bfloat16).reshape(row_count, heads_here, head_width)
    value_proj = projected[2].astype(jnp.bfloat16).reshape(row_count, heads_here, head_width)
    grad_heads = out_grad.reshape(row_count, heads_here, head_width)
    onehot = (table_rows[:, None] == jnp.arange(table_size, dtype=jnp.int32)[None, :]).astype(
        jnp.float32
    )
    table_flat = jnp.transpose(level_table, (1, 0, 2)).reshape(table_size, heads_here * level_count)
    lam = jnp.dot(onehot, table_flat, precision=highest).reshape(row_count, heads_here, level_count)
    local_state = jnp.einsum(
        "thd,the->hde", key_proj, value_proj, preferred_element_type=jnp.float32
    )
    block_sum = local_state
    level_list = []
    for bit_num in range(outer_bits):
        sibling = from_partner(block_sum, "ctx", bit_num)
        is_upper = jnp.right_shift(my_index, bit_num) & 1 == 1
        level_list.append(jnp.where(is_upper, sibling, 0.0))
        block_sum = block_sum + sibling
    level_states = jnp.stack(level_list)
    state_narrow = level_states.astype(jnp.bfloat16)
    far_out = jnp.zeros((row_count, heads_here, head_width), jnp.float32)
    query_far = jnp.zeros((row_count, heads_here, head_width), jnp.float32)
    grad_list = []
    for bit_num in range(outer_bits):
        level_weight = lam[:, :, inner_bits + 1 + bit_num]
        far_out = far_out + scale_factor * level_weight[..., None] * jnp.einsum(
            "thd,hde->the", queries, state_narrow[bit_num], preferred_element_type=jnp.float32
        )
        query_far = query_far + scale_factor * level_weight[..., None] * jnp.einsum(
            "the,hde->thd", grad_heads, state_narrow[bit_num], preferred_element_type=jnp.float32
        )
        scaled_query = ((scale_factor * level_weight)[..., None] * queries).astype(jnp.bfloat16)
        grad_list.append(
            jnp.einsum("thd,the->hde", scaled_query, grad_heads, preferred_element_type=jnp.float32)
        )
    pending = jnp.stack(grad_list)
    incoming = jnp.zeros((heads_here, head_width, head_width), jnp.float32)
    for bit_num in range(outer_bits):
        partner = from_partner(pending[bit_num:], "ctx", bit_num)
        is_lower = jnp.right_shift(my_index, bit_num) & 1 == 0
        incoming = incoming + jnp.where(is_lower, partner[0], 0.0)
        pending = jnp.concatenate(
            [pending[: bit_num + 1], pending[bit_num + 1 :] + partner[1:]], axis=0
        )
    back_state = incoming.astype(jnp.bfloat16)
    key_far = jnp.einsum("the,hde->thd", value_proj, back_state, preferred_element_type=jnp.float32)
    value_far = jnp.einsum("thd,hde->the", key_proj, back_state, preferred_element_type=jnp.float32)
    positions = jnp.arange(row_count, dtype=jnp.int32)
    pair_level = level_of(jnp.bitwise_xor(positions[:, None], positions[None, :]), inner_bits + 1)
    causal = positions[:, None] >= positions[None, :]
    near_outs = []
    query_nears = []
    key_nears = []
    value_nears = []
    for head_idx in range(heads_here):
        level_mix = jnp.zeros((row_count, row_count), jnp.float32)
        for level_num in range(inner_bits + 1):
            level_mix = jnp.where(
                pair_level == level_num, lam[:, head_idx, level_num][:, None], level_mix
            )
        level_mix = jnp.where(causal, level_mix * scale_factor, 0.0)
        query_head = queries[:, head_idx]
        key_head = key_proj[:, head_idx]
        value_head = value_proj[:, head_idx]
        grad_head = grad_heads[:, head_idx]
        scores = jnp.dot(query_head, key_head.T, preferred_element_type=jnp.float32)
        attn_probs = (level_mix * scores).astype(jnp.bfloat16)
        near_outs.append(jnp.dot(attn_probs, value_head, preferred_element_type=jnp.float32))
        grad_scores = jnp.dot(grad_head, value_head.T, preferred_element_type=jnp.float32)
        grad_mixed = (level_mix * grad_scores).astype(jnp.bfloat16)
        query_nears.append(jnp.dot(grad_mixed, key_head, preferred_element_type=jnp.float32))
        key_nears.append(jnp.dot(grad_mixed.T, query_head, preferred_element_type=jnp.float32))
        value_nears.append(jnp.dot(attn_probs.T, grad_head, preferred_element_type=jnp.float32))
    attended = (
        (jnp.stack(near_outs, axis=1) + far_out)
        .astype(jnp.bfloat16)
        .reshape(row_count, column_count)
    )
    query_total = (
        (jnp.stack(query_nears, axis=1) + query_far)
        .astype(jnp.bfloat16)
        .reshape(row_count, column_count)
    )
    key_total = (
        (jnp.stack(key_nears, axis=1) + key_far)
        .astype(jnp.bfloat16)
        .reshape(row_count, column_count)
    )
    value_total = (
        (jnp.stack(value_nears, axis=1) + value_far)
        .astype(jnp.bfloat16)
        .reshape(row_count, column_count)
    )
    merged = jnp.concatenate([query_total, key_total, value_total], axis=1)
    feature_cols = features
    grad_all = lax.psum_scatter(
        jnp.dot(feature_cols.T, merged, preferred_element_type=jnp.float32),
        "ctx",
        scatter_dimension=0,
        tiled=True,
    )
    grad_query = grad_all[:, :column_count]
    grad_key = grad_all[:, column_count : 2 * column_count]
    grad_value = grad_all[:, 2 * column_count :]
    return (attended, grad_query, grad_key, grad_value)


def solution(mesh):
    return jax.shard_map(
        on_device,
        mesh=mesh,
        in_specs=(
            P("ctx", "head"),
            P("ctx", "head"),
            P("ctx", "head"),
            P("ctx", "head"),
            P("head", None, None),
            P("ctx"),
            P("ctx", "head"),
        ),
        out_specs=(P("ctx", "head"), P("ctx", "head"), P("ctx", "head"), P("ctx", "head")),
        check_vma=False,
    )
```

profile of v0, /device:TPU:0, one launch (start us, length us, event | category | flops | bytes accessed | tf_op | source)
XLA Modules:
  0.0 552.1 jit_solution(5934484398656798456)
XLA Ops:
  14.7 47.3 %all-gather.9.cloned.1.call-done = bf16[2048,512]{1,0:T(8,128)(2,1)} async-done(((bf16[256,512]{1,0:T(8,128)(2,1)}), bf16[2048,512]{1,0:T(8,128)(2,1)}) %all-gather.9.cloned.1.call-update) | async-done | bytes 2097168 | tf_op jit(solution)/shard_map/all_gather | solution.py:40
  61.9 34.6 %all-gather.5.cloned.1.call-done = bf16[1024,2048]{1,0:T(8,128)(2,1)} async-done(((bf16[1024,512]{1,0:T(8,128)(2,1)}), bf16[1024,2048]{1,0:T(8,128)(2,1)}) %all-gather.5.cloned.1.call-update) | async-done | bytes 4194320 | tf_op jit(solution)/shard_map/all_gather | solution.py:26
  96.5 5.2 convolution_convert_fusion.1
  101.8 46.0 %all-gather.11.cloned.1.call-done = bf16[2048,512]{1,0:T(8,128)(2,1)} async-done(((bf16[256,512]{1,0:T(8,128)(2,1)}), bf16[2048,512]{1,0:T(8,128)(2,1)}) %all-gather.11.cloned.1.call-update) | async-done | bytes 2097168 | tf_op jit(solution)/shard_map/all_gather | solution.py:41
  147.8 5.2 convolution_convert_fusion
  153.0 9.0 %fusion = bf16[1024,1024]{1,0:T(8,128)(2,1)S(1)} fusion(f32[1024]{0:T(1024)S(1)} %bitcast.392, f32[1024]{0:T(1024)S(1)} %bitcast.394, f32[1024]{0:T(1024)S(1)} %bitcast.396, f32[1024]{0:T(1024)S(1)} %bitcast.398, f32[1024]{0:T(1024)S(1)} %bitcast.400, f32[1024]{0:T(1024)S(1)} %bitcast.402, f32[1024]{0:T(1024)S(1)} %bitcast.404, f32[1024]{0:T(1024)S(1)} %bitcast.406, ...), kind=kOutput, calls=%fused_computation.2 | convolution fusion | flops 331350016 | bytes 2666496 | tf_op jit(solution)/shard_map/dot_general | solution.py:119
  163.4 1.6 convolution_bitcast_fusion.9
  166.2 31.2 %all-gather.7.cloned.1.call-done = bf16[2048,512]{1,0:T(8,128)(2,1)} async-done(((bf16[256,512]{1,0:T(8,128)(2,1)}), bf16[2048,512]{1,0:T(8,128)(2,1)}) %all-gather.7.cloned.1.call-update) | async-done | bytes 2097168 | tf_op jit(solution)/shard_map/all_gather | solution.py:39
  197.4 5.4 convolution_convert_fusion.2
  203.3 9.5 %multiply_convert_fusion = bf16[1024,1024]{1,0:T(8,128)(2,1)S(1)} fusion(f32[1024]{0:T(1024)S(1)} %bitcast.393, f32[1024]{0:T(1024)S(1)} %bitcast.395, f32[1024]{0:T(1024)S(1)} %bitcast.397, f32[1024]{0:T(1024)S(1)} %bitcast.399, f32[1024]{0:T(1024)S(1)} %bitcast.401, f32[1024]{0:T(1024)S(1)} %bitcast.403, f32[1024]{0:T(1024)S(1)} %bitcast.405, ...), kind=kOutput, calls=%fused_computation.9 | convolution fusion | flops 331350016 | bytes 2666496 | tf_op jit(solution)/shard_map/dot_general | solution.py:116
  212.8 9.0 %fusion.1 = bf16[1024,1024]{1,0:T(8,128)(2,1)S(1)} fusion(f32[1024]{0:T(1024)S(1)} %bitcast.378, f32[1024]{0:T(1024)S(1)} %bitcast.380, f32[1024]{0:T(1024)S(1)} %bitcast.382, f32[1024]{0:T(1024)S(1)} %bitcast.384, f32[1024]{0:T(1024)S(1)} %bitcast.386, f32[1024]{0:T(1024)S(1)} %bitcast.388, f32[1024]{0:T(1024)S(1)} %bitcast.390, f32[1024]{0:T(1024)S(1)} %bitcast.356, ...), kind=kOutput, calls=%fused_computation.4 | convolution fusion | flops 331350016 | bytes 2666496 | tf_op jit(solution)/shard_map/dot_general | solution.py:119
  223.1 9.0 %multiply_convert_fusion.1 = bf16[1024,1024]{1,0:T(8,128)(2,1)S(1)} fusion(f32[1024]{0:T(1024)S(1)} %bitcast.379, f32[1024]{0:T(1024)S(1)} %bitcast.381, f32[1024]{0:T(1024)S(1)} %bitcast.383, f32[1024]{0:T(1024)S(1)} %bitcast.385, f32[1024]{0:T(1024)S(1)} %bitcast.387, f32[1024]{0:T(1024)S(1)} %bitcast.389, f32[1024]{0:T(1024)S(1)} %bitcast.391, ...), kind=kOutput, calls=%fused_computation.11 | convolution fusion | flops 331350016 | bytes 2666496 | tf_op jit(solution)/shard_map/dot_general | solution.py:116
  232.1 9.0 %fusion.2 = bf16[1024,1024]{1,0:T(8,128)(2,1)S(1)} fusion(f32[1024]{0:T(1024)S(1)} %bitcast.334, f32[1024]{0:T(1024)S(1)} %bitcast.336, f32[1024]{0:T(1024)S(1)} %bitcast.338, f32[1024]{0:T(1024)S(1)} %bitcast.340, f32[1024]{0:T(1024)S(1)} %bitcast.342, f32[1024]{0:T(1024)S(1)} %bitcast.344, f32[1024]{0:T(1024)S(1)} %bitcast.346, f32[1024]{0:T(1024)S(1)} %bitcast.348, ...), kind=kOutput, calls=%fused_computation.6 | convolution fusion | flops 331350016 | bytes 2666496 | tf_op jit(solution)/shard_map/dot_general | solution.py:119
  241.1 9.2 %multiply_convert_fusion.2 = bf16[1024,1024]{1,0:T(8,128)(2,1)S(1)} fusion(f32[1024]{0:T(1024)S(1)} %bitcast.335, f32[1024]{0:T(1024)S(1)} %bitcast.337, f32[1024]{0:T(1024)S(1)} %bitcast.339, f32[1024]{0:T(1024)S(1)} %bitcast.341, f32[1024]{0:T(1024)S(1)} %bitcast.343, f32[1024]{0:T(1024)S(1)} %bitcast.345, f32[1024]{0:T(1024)S(1)} %bitcast.347, ...), kind=kOutput, calls=%fused_computation.13 | convolution fusion | flops 331350016 | bytes 2666496 | tf_op jit(solution)/shard_map/dot_general | solution.py:116
  250.3 9.0 %fusion.3 = bf16[1024,1024]{1,0:T(8,128)(2,1)S(1)} fusion(f32[1024]{0:T(1024)S(1)} %bitcast.328, f32[1024]{0:T(1024)S(1)} %bitcast.330, f32[1024]{0:T(1024)S(1)} %bitcast.332, f32[1024]{0:T(1024)S(1)} %bitcast.368, f32[1024]{0:T(1024)S(1)} %bitcast.370, f32[1024]{0:T(1024)S(1)} %bitcast.372, f32[1024]{0:T(1024)S(1)} %bitcast.374, f32[1024]{0:T(1024)S(1)} %bitcast.376, ...), kind=kOutput, calls=%fused_computation.8 | convolution fusion | flops 331350016 | bytes 2666496 | tf_op jit(solution)/shard_map/dot_general | solution.py:119
  259.3 9.2 %multiply_convert_fusion.3 = bf16[1024,1024]{1,0:T(8,128)(2,1)S(1)} fusion(f32[1024]{0:T(1024)S(1)} %bitcast.329, f32[1024]{0:T(1024)S(1)} %bitcast.331, f32[1024]{0:T(1024)S(1)} %bitcast.333, f32[1024]{0:T(1024)S(1)} %bitcast.369, f32[1024]{0:T(1024)S(1)} %bitcast.371, f32[1024]{0:T(1024)S(1)} %bitcast.373, f32[1024]{0:T(1024)S(1)} %bitcast.375, ...), kind=kOutput, calls=%fused_computation.15 | convolution fusion | flops 331350016 | bytes 2666496 | tf_op jit(solution)/shard_map/dot_general | solution.py:116
  279.4 12.2 %collective-permute-done.3 = f32[3,4,128,128]{3,2,1,0:T(8,128)S(1)} collective-permute-done((f32[3,4,128,128]{3,2,1,0:T(8,128)S(1)}, f32[3,4,128,128]{3,2,1,0:T(8,128)S(1)}, u32[]{:S(2)}, u32[]{:S(2)}) %collective-permute-start.3) | collective-permute-done | bytes 786464 | tf_op jit(solution)/shard_map/ppermute | solution.py:15
  291.7 2.4 collective-permute-start.4
  296.5 10.4 %collective-permute-done.4 = f32[2,4,128,128]{3,2,1,0:T(8,128)S(1)} collective-permute-done((f32[2,4,128,128]{3,2,1,0:T(8,128)S(1)}, f32[2,4,128,128]{3,2,1,0:T(8,128)S(1)}, u32[]{:S(2)}, u32[]{:S(2)}) %collective-permute-start.4) | collective-permute-done | bytes 524320 | tf_op jit(solution)/shard_map/ppermute | solution.py:15
  309.3 11.1 %collective-permute-done.5 = f32[1,4,128,128]{3,2,1,0:T(8,128)S(1)} collective-permute-done((f32[1,4,128,128]{3,2,1,0:T(8,128)S(1)}, f32[1,4,128,128]{3,2,1,0:T(8,128)S(1)}, u32[]{:S(2)}, u32[]{:S(2)}) %collective-permute-start.5) | collective-permute-done | bytes 262176 | tf_op jit(solution)/shard_map/ppermute | solution.py:15
  322.6 12.2 %convolution_bitcast_fusion = f32[2048,1536]{0,1:T(8,128)} fusion(bf16[1024,2048]{1,0:T(8,128)(2,1)S(1)} %copy-done.19, bf16[1024,512]{0,1:T(8,128)(2,1)S(1)} %bitcast.415, bf16[1024,512]{0,1:T(8,128)(2,1)S(1)} %bitcast.414, bf16[1024,512]{0,1:T(8,128)(2,1)S(1)} %bitcast.320), kind=kOutput, calls=%fused_computation | convolution fusion | flops 6451888128 | bytes 19922944 | tf_op jit(solution)/shard_map/dot_general | solution.py:147
  334.8 2.6 convolution_bitcast_fusion.13
  337.4 2.4 convolution_bitcast_fusion.14
  344.8 196.1 %reduce-scatter.2.cloned.1.call-done = f32[256,1536]{0,1:T(8,128)} async-done(((f32[2048,1536]{0,1:T(8,128)}), f32[256,1536]{0,1:T(8,128)}) %reduce-scatter.2.cloned.1.call-update) | async-done | bytes 1572880 | tf_op jit(solution)/shard_map/reduce_scatter | solution.py:146
  (105 shorter events, 38.7 us)
Async XLA Ops:
  7.2 54.8 %all-gather.9.cloned.1.call-start = ((), (), s32[]{:S(2)}) async-start(), calls=%async_computation.3 | async-start | bytes 2359296 | tf_op jit(solution)/shard_map/all_gather | solution.py:40
  7.9 88.6 %all-gather.5.cloned.1.call-start = ((), (), s32[]{:S(2)}) async-start(), calls=%async_computation.1 | async-start | bytes 5242880 | tf_op jit(solution)/shard_map/all_gather | solution.py:26
  8.6 139.1 %all-gather.11.cloned.1.call-start = ((), (), s32[]{:S(2)}) async-start(), calls=%async_computation.4 | async-start | bytes 2359296 | tf_op jit(solution)/shard_map/all_gather | solution.py:41
  9.4 188.0 %all-gather.7.cloned.1.call-start = ((), (), s32[]{:S(2)}) async-start(), calls=%async_computation.2 | async-start | bytes 2359296 | tf_op jit(solution)/shard_map/all_gather | solution.py:39
  10.0 530.9 %reduce-scatter.2.cloned.1.call-start = ((), (), s32[]{:S(2)}) async-start(), calls=%async_computation.5 | async-start | bytes 14155776 | tf_op jit(solution)/shard_map/reduce_scatter | solution.py:146
  101.8 63.3 %copy-start.8 = (bf16[1024,512]{0,1:T(8,128)(2,1)}, bf16[1024,512]{0,1:T(8,128)(2,1)S(1)}, u32[]{:S(2)}) copy-start(bf16[1024,512]{0,1:T(8,128)(2,1)S(1)} %convolution_convert_fusion.1) | copy-start | bytes 3145732
  197.4 5.4 copy-start.7
  197.4 5.8 %copy-start.9 = (bf16[1024,512]{0,1:T(8,128)(2,1)S(1)}, bf16[1024,512]{0,1:T(8,128)(2,1)}, u32[]{:S(2)}) copy-start(bf16[1024,512]{0,1:T(8,128)(2,1)} %copy-done.8) | copy-start | bytes 3145732
  212.8 59.3 %copy-start = (bf16[1024,1024]{1,0:T(8,128)(2,1)}, bf16[1024,1024]{1,0:T(8,128)(2,1)S(1)}, u32[]{:S(2)}) copy-start(bf16[1024,1024]{1,0:T(8,128)(2,1)S(1)} %multiply_convert_fusion) | copy-start | bytes 6291460
  232.1 40.5 %copy-start.1 = (bf16[1024,1024]{1,0:T(8,128)(2,1)}, bf16[1024,1024]{1,0:T(8,128)(2,1)S(1)}, u32[]{:S(2)}) copy-start(bf16[1024,1024]{1,0:T(8,128)(2,1)S(1)} %multiply_convert_fusion.1) | copy-start | bytes 6291460
  250.3 23.2 %copy-start.2 = (bf16[1024,1024]{1,0:T(8,128)(2,1)}, bf16[1024,1024]{1,0:T(8,128)(2,1)S(1)}, u32[]{:S(2)}) copy-start(bf16[1024,1024]{1,0:T(8,128)(2,1)S(1)} %multiply_convert_fusion.2) | copy-start | bytes 6291460
  259.3 9.2 %copy-start.13 = (f32[4,128,128]{2,1,0:T(8,128)S(1)}, f32[4,128,128]{2,1,0:T(8,128)}, u32[]{:S(2)}) copy-start(f32[4,128,128]{2,1,0:T(8,128)} %fusion.60) | copy-start | bytes 786436
  259.3 9.9 %copy-start.15 = (f32[1024,4]{0,1:T(4,128)S(1)}, f32[1024,4]{0,1:T(4,128)}, u32[]{:S(2)}) copy-start(f32[1024,4]{0,1:T(4,128)} %get-tuple-element.66) | copy-start | bytes 49156
  259.3 10.3 %copy-start.17 = (f32[1024,4]{0,1:T(4,128)S(1)}, f32[1024,4]{0,1:T(4,128)}, u32[]{:S(2)}) copy-start(f32[1024,4]{0,1:T(4,128)} %get-tuple-element.67) | copy-start | bytes 49156
  268.5 6.8 %copy-start.4 = (bf16[1024,1024]{1,0:T(8,128)(2,1)}, bf16[1024,1024]{1,0:T(8,128)(2,1)S(1)}, u32[]{:S(2)}) copy-start(bf16[1024,1024]{1,0:T(8,128)(2,1)S(1)} %multiply_convert_fusion.3) | copy-start | bytes 6291460
  268.5 9.2 %collective-permute-start = (f32[4,128,128]{2,1,0:T(8,128)S(1)}, f32[4,128,128]{2,1,0:T(8,128)S(1)}, u32[]{:S(2)}, u32[]{:S(2)}) collective-permute-start(f32[4,128,128]{2,1,0:T(8,128)S(1)} %copy-done.13), channel_id=1, source_target_pairs={{0,4},{4,0},{8,12},{12,8},{16,20},{20,16},{24,28},{28,24},{1,5},{5... | collective-permute-start | bytes 786440 | tf_op jit(solution)/shard_map/ppermute | solution.py:15
  270.6 21.0 %collective-permute-start.3 = (f32[3,4,128,128]{3,2,1,0:T(8,128)S(1)}, f32[3,4,128,128]{3,2,1,0:T(8,128)S(1)}, u32[]{:S(2)}, u32[]{:S(2)}) collective-permute-start(f32[3,4,128,128]{3,2,1,0:T(8,128)S(1)} %pad_maximum_fusion), channel_id=1, source_target_pairs={{0,4},{4,0},{8,12},{12,8},{16,20},{20,16},{24,28},{28,24},{1,5},{5... | collective-permute-start | bytes 2359304 | tf_op jit(solution)/shard_map/ppermute | solution.py:15
  277.8 16.7 %collective-permute-start.1 = (f32[4,128,128]{2,1,0:T(8,128)S(1)}, f32[4,128,128]{2,1,0:T(8,128)S(1)}, u32[]{:S(2)}, u32[]{:S(2)}) collective-permute-start(f32[4,128,128]{2,1,0:T(8,128)S(1)} %add.946), channel_id=1, source_target_pairs={{0,8},{8,0},{4,12},{12,4},{16,24},{24,16},{20,28},{28,20},{1,9},{9... | collective-permute-start | bytes 786440 | tf_op jit(solution)/shard_map/ppermute | solution.py:15
  291.7 16.7 %copy-start.12 = (f32[1024,1,128]{0,2,1:T(8,128)S(1)}, f32[1024,1,128]{0,2,1:T(8,128)}, u32[]{:S(2)}) copy-start(f32[1024,1,128]{0,2,1:T(8,128)} %convolution_bitcast_fusion.9) | copy-start | bytes 1572868
  291.7 15.2 %collective-permute-start.4 = (f32[2,4,128,128]{3,2,1,0:T(8,128)S(1)}, f32[2,4,128,128]{3,2,1,0:T(8,128)S(1)}, u32[]{:S(2)}, u32[]{:S(2)}) collective-permute-start(f32[2,4,128,128]{3,2,1,0:T(8,128)S(1)} %slice_add_fusion), channel_id=1, source_target_pairs={{0,8},{8,0},{4,12},{12,4},{16,24},{24,16},{20,28},{28,20},{1,9},{9... | collective-permute-start | bytes 1572872 | tf_op jit(solution)/shard_map/ppermute | solution.py:15
  294.5 14.7 %copy-start.10 = (f32[4,128,128]{2,1,0:T(8,128)}, f32[4,128,128]{2,1,0:T(8,128)S(1)}, u32[]{:S(2)}) copy-start(f32[4,128,128]{2,1,0:T(8,128)S(1)} %collective-permute-done.1) | copy-start | bytes 786436
  294.6 13.8 %collective-permute-start.2 = (bf16[4,128,128]{2,1,0:T(8,128)(2,1)S(1)}, bf16[4,128,128]{2,1,0:T(8,128)(2,1)S(1)}, u32[]{:S(2)}, u32[]{:S(2)}) collective-permute-start(bf16[4,128,128]{2,1,0:T(8,128)(2,1)S(1)} %add.948), channel_id=1, source_target_pairs={{0,16},{16,0},{4,20},{20,4},{8,24},{24,8},{12,28},{28,12},{1,17},{... | collective-permute-start | bytes 393224 | tf_op jit(solution)/shard_map/ppermute | solution.py:15
  306.9 13.4 %collective-permute-start.5 = (f32[1,4,128,128]{3,2,1,0:T(8,128)S(1)}, f32[1,4,128,128]{3,2,1,0:T(8,128)S(1)}, u32[]{:S(2)}, u32[]{:S(2)}) collective-permute-start(f32[1,4,128,128]{3,2,1,0:T(8,128)S(1)} %slice_add_fusion.1), channel_id=1, source_target_pairs={{0,16},{16,0},{4,20},{20,4},{8,24},{24,8},{12,28},{28,12},{1,17},{... | collective-permute-start | bytes 786440 | tf_op jit(solution)/shard_map/ppermute | solution.py:15
  334.8 5.9 %copy-start.5 = (bf16[1024,1024]{1,0:T(8,128)(2,1)S(1)}, bf16[1024,1024]{1,0:T(8,128)(2,1)}, u32[]{:S(2)}) copy-start(bf16[1024,1024]{1,0:T(8,128)(2,1)} %copy-done.4) | copy-start | bytes 6291460
  (7 other events, 16.0 us)
Sparse Core Ops, SparseCore 0:
  10.1 51.7 all-gather.8
  63.5 32.9 all-gather.4
  98.7 49.0 all-gather.10
  149.8 47.6 all-gather.6
  334.9 205.8 reduce-scatter.1
where the time goes:
time: 560 us; the launch traced here: 552 us
  waiting for transfers between devices  393 us (70%)
  matrix products  123 us (22%)
  between operations  14.7 us (3%)
  local copies, waits for them, and re-layouts  12.1 us (2%)
  starting transfers between devices  9.27 us (2%)
    reduce_scatter x1, waiting for transfers between devices, on_device(): lax.psum_scatter(jnp.dot(feature_cols.T, merged, preferred_element_type=j...  196 us
    all_gather x1, waiting for transfers between devices, on_device(): lax.all_gather(w_key, 'ctx', axis=0, tiled=True)  47.3 us
    all_gather x1, waiting for transfers between devices, on_device(): lax.all_gather(w_value, 'ctx', axis=0, tiled=True)  46 us
    dot_general x4, matrix products, on_device(): scores = jnp.dot(query_head, key_head.T, preferred_element_type=jnp.float32)  36.9 us
    dot_general x4, matrix products, on_device(): jnp.dot(grad_head, value_head.T, preferred_element_type=jnp.float32)  35.9 us
    ppermute x6, waiting for transfers between devices, from_partner(): return lax.ppermute(block, axis, route)  34.8 us
    all_gather x1, waiting for transfers between devices, on_device(): features = lax.all_gather(activations, 'head', axis=1, tiled=True)  34.6 us
    all_gather x1, waiting for transfers between devices, on_device(): lax.all_gather(w_query, 'ctx', axis=0, tiled=True)  31.2 us
  transfers between devices with their start and end apart: 11, of which 9 were waited for; matrix products, arithmetic and copies ran while one was open for 8% of the time, Pallas kernels for 0%

commit v1 on v0

--- a/solution.py
+++ b/solution.py
@@ -3,6 +3,17 @@
 import jax.numpy as jnp
 from jax import lax
 from jax.sharding import PartitionSpec as P
+
+
+def around_the_ring(shard, axis, dim):
+    n_dev = lax.axis_size(axis)
+    forward = [(i, (i + 1) % n_dev) for i in range(n_dev)]
+    parts = [shard]
+    for far in range(1, n_dev):
+        parts = [lax.ppermute(parts[0], axis, forward), *parts]
+    out = jnp.concatenate(parts, axis=dim)
+    turn = (lax.axis_index(axis) + 1) * parts[-1].shape[dim]
+    return jnp.roll(out, turn, axis=dim)
 
 
 def from_partner(block, axis, apart):
@@ -23,7 +34,7 @@
 
 
 def on_device(activations, w_query, w_key, w_value, level_table, table_rows, out_grad):
-    features = lax.all_gather(activations, "head", axis=1, tiled=True)
+    features = around_the_ring(activations, "head", 1)
     row_count = features.shape[0]
     column_count = w_query.shape[1]
     heads_here = level_table.shape[0]

time: 560 us -> 534 us (0.954)
  waiting for transfers between devices: 393 us -> 354 us
  local copies, waits for them, and re-layouts: 12.1 us -> 22.7 us
    all_gather x1, waiting for transfers between devices: 47.3 us -> 0.01 us  [on_device(): lax.all_gather(w_key, 'ctx', axis=0, tiled=True)]
    ppermute x0 -> x3, waiting for transfers between devices: none -> 37.3 us  [around_the_ring(): parts = [lax.ppermute(parts[0], axis, forward), *parts]]
    all_gather x1 -> x0, waiting for transfers between devices: 34.6 us -> none  [on_device(): features = lax.all_gather(activations, 'head', axis=1, tiled=True)]
    all_gather x1, waiting for transfers between devices: 31.2 us -> 43.4 us  [on_device(): lax.all_gather(w_query, 'ctx', axis=0, tiled=True)]
    unnamed x47 -> x61, local copies, waits for them, and re-layouts: 9.71 us -> 17 us
    all_gather x1, waiting for transfers between devices: 46 us -> 40 us  [on_device(): lax.all_gather(w_value, 'ctx', axis=0, tiled=True)]
  transfers between devices with their start and end apart: 11 -> 13, of which waited for: 9 -> 10; matrix products, arithmetic and copies ran while one was open for 8% -> 9% of each run, Pallas kernels for 0% -> 0%
where the time goes in v1:
time: 534 us; the launch traced here: 525 us
  waiting for transfers between devices  354 us (66%)
  matrix products  124 us (23%)
  local copies, waits for them, and re-layouts  22.7 us (4%)
  between operations  14.9 us (3%)
  starting transfers between devices  9.69 us (2%)
    reduce_scatter x1, waiting for transfers between devices, on_device(): lax.psum_scatter(jnp.dot(feature_cols.T, merged, preferred_element_type=j...  197 us
    all_gather x1, waiting for transfers between devices, on_device(): lax.all_gather(w_query, 'ctx', axis=0, tiled=True)  43.4 us
    all_gather x1, waiting for transfers between devices, on_device(): lax.all_gather(w_value, 'ctx', axis=0, tiled=True)  40 us
    ppermute x3, waiting for transfers between devices, around_the_ring(): parts = [lax.ppermute(parts[0], axis, forward), *parts]  37.3 us
    dot_general x4, matrix products, on_device(): scores = jnp.dot(query_head, key_head.T, preferred_element_type=jnp.float32)  36.1 us
    dot_general x4, matrix products, on_device(): jnp.dot(grad_head, value_head.T, preferred_element_type=jnp.float32)  36.1 us
    ppermute x6, waiting for transfers between devices, from_partner(): return lax.ppermute(block, axis, route)  35.1 us
    unnamed x61, local copies, waits for them, and re-layouts  17 us
  transfers between devices with their start and end apart: 13, of which 10 were waited for; matrix products, arithmetic and copies ran while one was open for 9% of the time, Pallas kernels for 0%

profile of v1, /device:TPU:0, one launch (start us, length us, event | category | flops | bytes accessed | tf_op | source)
XLA Modules:
  0.0 525.0 jit_solution(8760333317998196761)
XLA Ops:
  9.2 14.6 %collective-permute-done = bf16[1024,512]{1,0:T(8,128)(2,1)S(1)} collective-permute-done((bf16[1024,512]{1,0:T(8,128)(2,1)}, bf16[1024,512]{1,0:T(8,128)(2,1)S(1)}, u32[]{:S(2)}, u32[]{:S(2)}) %collective-permute-start) | collective-permute-done | bytes 1048608 | tf_op jit(solution)/shard_map/ppermute | solution.py:13
  25.7 12.5 %collective-permute-done.1 = bf16[1024,512]{1,0:T(8,128)(2,1)} collective-permute-done((bf16[1024,512]{1,0:T(8,128)(2,1)S(1)}, bf16[1024,512]{1,0:T(8,128)(2,1)}, u32[]{:S(2)}, u32[]{:S(2)}) %collective-permute-start.1) | collective-permute-done | bytes 1048608 | tf_op jit(solution)/shard_map/ppermute | solution.py:13
  42.5 10.2 %collective-permute-done.2 = bf16[1024,512]{1,0:T(8,128)(2,1)} collective-permute-done((bf16[1024,512]{1,0:T(8,128)(2,1)}, bf16[1024,512]{1,0:T(8,128)(2,1)}, u32[]{:S(2)}, u32[]{:S(2)}) %collective-permute-start.2) | collective-permute-done | bytes 1048608 | tf_op jit(solution)/shard_map/ppermute | solution.py:13
  66.5 5.2 fusion.42
  71.7 40.0 %all-gather.8.cloned.1.call-done = bf16[2048,512]{1,0:T(8,128)(2,1)} async-done(((bf16[256,512]{1,0:T(8,128)(2,1)}), bf16[2048,512]{1,0:T(8,128)(2,1)}) %all-gather.8.cloned.1.call-update) | async-done | bytes 2097168 | tf_op jit(solution)/shard_map/all_gather | solution.py:52
  111.7 5.2 fusion.45
  118.1 43.4 %all-gather.4.cloned.1.call-done = bf16[2048,512]{1,0:T(8,128)(2,1)} async-done(((bf16[256,512]{1,0:T(8,128)(2,1)}), bf16[2048,512]{1,0:T(8,128)(2,1)}) %all-gather.4.cloned.1.call-update) | async-done | bytes 2097168 | tf_op jit(solution)/shard_map/all_gather | solution.py:50
  161.5 5.3 %fusion.39 = bf16[1024,512]{0,1:T(8,128)(2,1)S(1)} fusion(bf16[2048,512]{1,0:T(8,128)(2,1)} %all-gather.4.cloned.1.call-done, bf16[1024,4096]{1,0:T(8,128)(2,1)} %constant_dynamic-update-slice_fusion, s32[]{:T(128)S(6)} %select_n.213), kind=kOutput, calls=%fused_computation.78 | convolution fusion | flops 2148007936 | bytes 7340036 | tf_op jit(solution)/shard_map/dot_general | solution.py:57
  166.9 9.0 %multiply_convert_fusion = bf16[1024,1024]{1,0:T(8,128)(2,1)S(1)} fusion(f32[1024]{0:T(1024)S(1)} %bitcast.378, f32[1024]{0:T(1024)S(1)} %bitcast.380, f32[1024]{0:T(1024)S(1)} %bitcast.382, f32[1024]{0:T(1024)S(1)} %bitcast.384, f32[1024]{0:T(1024)S(1)} %bitcast.386, f32[1024]{0:T(1024)S(1)} %bitcast.388, f32[1024]{0:T(1024)S(1)} %bitcast.390, ...), kind=kOutput, calls=%fused_computation.8 | convolution fusion | flops 331350016 | bytes 2666496 | tf_op jit(solution)/shard_map/dot_general | solution.py:127
  175.9 9.2 %fusion = bf16[1024,1024]{1,0:T(8,128)(2,1)S(1)} fusion(f32[1024]{0:T(1024)S(1)} %bitcast.379, f32[1024]{0:T(1024)S(1)} %bitcast.381, f32[1024]{0:T(1024)S(1)} %bitcast.383, f32[1024]{0:T(1024)S(1)} %bitcast.385, f32[1024]{0:T(1024)S(1)} %bitcast.387, f32[1024]{0:T(1024)S(1)} %bitcast.389, f32[1024]{0:T(1024)S(1)} %bitcast.391, f32[1024]{0:T(1024)S(1)} %bitcast.393, ...), kind=kOutput, calls=%fused_computation.1 | convolution fusion | flops 331350016 | bytes 2666496 | tf_op jit(solution)/shard_map/dot_general | solution.py:130
  185.1 9.0 %multiply_convert_fusion.1 = bf16[1024,1024]{1,0:T(8,128)(2,1)S(1)} fusion(f32[1024]{0:T(1024)S(1)} %bitcast.342, f32[1024]{0:T(1024)S(1)} %bitcast.344, f32[1024]{0:T(1024)S(1)} %bitcast.346, f32[1024]{0:T(1024)S(1)} %bitcast.348, f32[1024]{0:T(1024)S(1)} %bitcast.350, f32[1024]{0:T(1024)S(1)} %bitcast.352, f32[1024]{0:T(1024)S(1)} %bitcast.354, ...), kind=kOutput, calls=%fused_computation.10 | convolution fusion | flops 331350016 | bytes 2666496 | tf_op jit(solution)/shard_map/dot_general | solution.py:127
  194.1 9.0 %fusion.1 = bf16[1024,1024]{1,0:T(8,128)(2,1)S(1)} fusion(f32[1024]{0:T(1024)S(1)} %bitcast.343, f32[1024]{0:T(1024)S(1)} %bitcast.345, f32[1024]{0:T(1024)S(1)} %bitcast.347, f32[1024]{0:T(1024)S(1)} %bitcast.349, f32[1024]{0:T(1024)S(1)} %bitcast.351, f32[1024]{0:T(1024)S(1)} %bitcast.353, f32[1024]{0:T(1024)S(1)} %bitcast.355, f32[1024]{0:T(1024)S(1)} %bitcast.401, ...), kind=kOutput, calls=%fused_computation.3 | convolution fusion | flops 331350016 | bytes 2666496 | tf_op jit(solution)/shard_map/dot_general | solution.py:130
  203.1 9.0 %multiply_convert_fusion.2 = bf16[1024,1024]{1,0:T(8,128)(2,1)S(1)} fusion(f32[1024]{0:T(1024)S(1)} %bitcast.356, f32[1024]{0:T(1024)S(1)} %bitcast.358, f32[1024]{0:T(1024)S(1)} %bitcast.360, f32[1024]{0:T(1024)S(1)} %bitcast.362, f32[1024]{0:T(1024)S(1)} %bitcast.364, f32[1024]{0:T(1024)S(1)} %bitcast.366, f32[1024]{0:T(1024)S(1)} %bitcast.368, ...), kind=kOutput, calls=%fused_computation.12 | convolution fusion | flops 331350016 | bytes 2666496 | tf_op jit(solution)/shard_map/dot_general | solution.py:127
  212.1 9.0 %fusion.2 = bf16[1024,1024]{1,0:T(8,128)(2,1)S(1)} fusion(f32[1024]{0:T(1024)S(1)} %bitcast.357, f32[1024]{0:T(1024)S(1)} %bitcast.359, f32[1024]{0:T(1024)S(1)} %bitcast.361, f32[1024]{0:T(1024)S(1)} %bitcast.363, f32[1024]{0:T(1024)S(1)} %bitcast.365, f32[1024]{0:T(1024)S(1)} %bitcast.367, f32[1024]{0:T(1024)S(1)} %bitcast.369, f32[1024]{0:T(1024)S(1)} %bitcast.371, ...), kind=kOutput, calls=%fused_computation.5 | convolution fusion | flops 331350016 | bytes 2666496 | tf_op jit(solution)/shard_map/dot_general | solution.py:130
  221.1 9.2 %multiply_convert_fusion.3 = bf16[1024,1024]{1,0:T(8,128)(2,1)S(1)} fusion(f32[1024]{0:T(1024)S(1)} %bitcast.336, f32[1024]{0:T(1024)S(1)} %bitcast.338, f32[1024]{0:T(1024)S(1)} %bitcast.340, f32[1024]{0:T(1024)S(1)} %bitcast.322, f32[1024]{0:T(1024)S(1)} %bitcast.324, f32[1024]{0:T(1024)S(1)} %bitcast.326, f32[1024]{0:T(1024)S(1)} %bitcast.328, ...), kind=kOutput, calls=%fused_computation.14 | convolution fusion | flops 331350016 | bytes 2666496 | tf_op jit(solution)/shard_map/dot_general | solution.py:127
  230.3 9.0 %fusion.3 = bf16[1024,1024]{1,0:T(8,128)(2,1)S(1)} fusion(f32[1024]{0:T(1024)S(1)} %bitcast.337, f32[1024]{0:T(1024)S(1)} %bitcast.339, f32[1024]{0:T(1024)S(1)} %bitcast.341, f32[1024]{0:T(1024)S(1)} %bitcast.323, f32[1024]{0:T(1024)S(1)} %bitcast.325, f32[1024]{0:T(1024)S(1)} %bitcast.327, f32[1024]{0:T(1024)S(1)} %bitcast.329, f32[1024]{0:T(1024)S(1)} %bitcast.331, ...), kind=kOutput, calls=%fused_computation.7 | convolution fusion | flops 331350016 | bytes 2666496 | tf_op jit(solution)/shard_map/dot_general | solution.py:130
  252.5 12.7 %collective-permute-done.6 = f32[3,4,128,128]{3,2,1,0:T(8,128)S(1)} collective-permute-done((f32[3,4,128,128]{3,2,1,0:T(8,128)S(1)}, f32[3,4,128,128]{3,2,1,0:T(8,128)S(1)}, u32[]{:S(2)}, u32[]{:S(2)}) %collective-permute-start.6) | collective-permute-done | bytes 786464 | tf_op jit(solution)/shard_map/ppermute | solution.py:26
  269.9 10.7 %collective-permute-done.7 = f32[2,4,128,128]{3,2,1,0:T(8,128)S(1)} collective-permute-done((f32[2,4,128,128]{3,2,1,0:T(8,128)S(1)}, f32[2,4,128,128]{3,2,1,0:T(8,128)S(1)}, u32[]{:S(2)}, u32[]{:S(2)}) %collective-permute-start.7) | collective-permute-done | bytes 524320 | tf_op jit(solution)/shard_map/ppermute | solution.py:26
  282.5 11.2 %collective-permute-done.8 = f32[1,4,128,128]{3,2,1,0:T(8,128)S(1)} collective-permute-done((f32[1,4,128,128]{3,2,1,0:T(8,128)S(1)}, f32[1,4,128,128]{3,2,1,0:T(8,128)S(1)}, u32[]{:S(2)}, u32[]{:S(2)}) %collective-permute-start.8) | collective-permute-done | bytes 262176 | tf_op jit(solution)/shard_map/ppermute | solution.py:26
  294.7 14.2 %fusion.15 = f32[2048,1536]{1,0:T(8,128)} fusion(bf16[1024,512]{0,1:T(8,128)(2,1)S(1)} %bitcast.408, bf16[1024,512]{0,1:T(8,128)(2,1)S(1)} %bitcast.409, bf16[1024,512]{0,1:T(8,128)(2,1)S(1)} %bitcast.314, bf16[1024,4096]{1,0:T(8,128)(2,1)} %constant_dynamic-update-slice_fusion, s32[]{:T(128)S(6)} %select_n.213), kind=kOutput, calls=%fused_computation.30 | convolution fusion | flops 6451888128 | bytes 19922948 | tf_op jit(solution)/shard_map/dot_general | solution.py:158
  309.0 2.6 convolution_bitcast_fusion.12
  311.5 2.4 convolution_bitcast_fusion.13
  318.9 196.6 %reduce-scatter.2.cloned.1.call-done = f32[256,1536]{1,0:T(8,128)} async-done(((f32[2048,1536]{1,0:T(8,128)}), f32[256,1536]{1,0:T(8,128)}) %reduce-scatter.2.cloned.1.call-update) | async-done | bytes 1572880 | tf_op jit(solution)/shard_map/reduce_scatter | solution.py:157
  515.5 2.5 fusion.77
  (123 shorter events, 48.5 us)
Async XLA Ops:
  7.2 59.3 %all-gather.6.cloned.1.call-start = ((), (), s32[]{:S(2)}) async-start(), calls=%async_computation.2 | async-start | bytes 2359296 | tf_op jit(solution)/shard_map/all_gather | solution.py:51
  7.9 103.8 %all-gather.8.cloned.1.call-start = ((), (), s32[]{:S(2)}) async-start(), calls=%async_computation.3 | async-start | bytes 2359296 | tf_op jit(solution)/shard_map/all_gather | solution.py:52
  8.6 152.9 %all-gather.4.cloned.1.call-start = ((), (), s32[]{:S(2)}) async-start(), calls=%async_computation.1 | async-start | bytes 2359296 | tf_op jit(solution)/shard_map/all_gather | solution.py:50
  8.7 15.2 %collective-permute-start = (bf16[1024,512]{1,0:T(8,128)(2,1)}, bf16[1024,512]{1,0:T(8,128)(2,1)S(1)}, u32[]{:S(2)}, u32[]{:S(2)}) collective-permute-start(bf16[1024,512]{1,0:T(8,128)(2,1)} %param.7), channel_id=1, source_target_pairs={{0,1},{1,2},{2,3},{3,0},{4,5},{5,6},{6,7},{7,4},{8,9},{9,10},{10,1... | collective-permute-start | bytes 3145736 | tf_op jit(solution)/shard_map/ppermute | solution.py:13
  23.9 14.3 %collective-permute-start.1 = (bf16[1024,512]{1,0:T(8,128)(2,1)S(1)}, bf16[1024,512]{1,0:T(8,128)(2,1)}, u32[]{:S(2)}, u32[]{:S(2)}) collective-permute-start(bf16[1024,512]{1,0:T(8,128)(2,1)S(1)} %collective-permute-done), channel_id=1, source_target_pairs={{0,1},{1,2},{2,3},{3,0},{4,5},{5,6},{6,7},{7,4},{8,9},{9,10},{10,1... | collective-permute-start | bytes 3145736 | tf_op jit(solution)/shard_map/ppermute | solution.py:13
  23.9 491.6 %reduce-scatter.2.cloned.1.call-start = ((), (), s32[]{:S(2)}) async-start(), calls=%async_computation.4 | async-start | bytes 14155776 | tf_op jit(solution)/shard_map/reduce_scatter | solution.py:157
  38.2 14.5 %collective-permute-start.2 = (bf16[1024,512]{1,0:T(8,128)(2,1)}, bf16[1024,512]{1,0:T(8,128)(2,1)}, u32[]{:S(2)}, u32[]{:S(2)}) collective-permute-start(bf16[1024,512]{1,0:T(8,128)(2,1)} %collective-permute-done.1), channel_id=1, source_target_pairs={{0,1},{1,2},{2,3},{3,0},{4,5},{5,6},{6,7},{7,4},{8,9},{9,10},{10,1... | collective-permute-start | bytes 3145736 | tf_op jit(solution)/shard_map/ppermute | solution.py:13
  38.9 19.7 %copy-start.6 = (bf16[1024,512]{1,0:T(8,128)(2,1)S(1)}, bf16[1024,512]{1,0:T(8,128)(2,1)}, u32[]{:S(2)}) copy-start(bf16[1024,512]{1,0:T(8,128)(2,1)} %param.7) | copy-start | bytes 3145732
  71.7 45.2 %copy-start.7 = (bf16[1024,512]{0,1:T(8,128)(2,1)}, bf16[1024,512]{0,1:T(8,128)(2,1)S(1)}, u32[]{:S(2)}) copy-start(bf16[1024,512]{0,1:T(8,128)(2,1)S(1)} %fusion.42) | copy-start | bytes 3145732
  118.1 48.7 %copy-start.17 = (f32[1024,1,1]{0,2,1:T(1,128)S(1)}, f32[1024,1,1]{0,2,1:T(1,128)}, u32[]{:S(2)}) copy-start(f32[1024,1,1]{0,2,1:T(1,128)} %get-tuple-element.30) | copy-start | bytes 12292
  118.1 48.7 %copy-start.18 = (f32[1024,1,1]{0,2,1:T(1,128)S(1)}, f32[1024,1,1]{0,2,1:T(1,128)}, u32[]{:S(2)}) copy-start(f32[1024,1,1]{0,2,1:T(1,128)} %get-tuple-element.31) | copy-start | bytes 12292
  118.1 48.7 %copy-start.19 = (f32[1024,1,1]{0,2,1:T(1,128)S(1)}, f32[1024,1,1]{0,2,1:T(1,128)}, u32[]{:S(2)}) copy-start(f32[1024,1,1]{0,2,1:T(1,128)} %get-tuple-element.32) | copy-start | bytes 12292
  118.1 48.7 %copy-start.20 = (f32[1024,1,1]{0,2,1:T(1,128)S(1)}, f32[1024,1,1]{0,2,1:T(1,128)}, u32[]{:S(2)}) copy-start(f32[1024,1,1]{0,2,1:T(1,128)} %get-tuple-element.33) | copy-start | bytes 12292
  175.9 66.7 %copy-start = (bf16[1024,1024]{1,0:T(8,128)(2,1)}, bf16[1024,1024]{1,0:T(8,128)(2,1)S(1)}, u32[]{:S(2)}) copy-start(bf16[1024,1024]{1,0:T(8,128)(2,1)S(1)} %multiply_convert_fusion) | copy-start | bytes 6291460
  194.1 48.9 %copy-start.1 = (bf16[1024,1024]{1,0:T(8,128)(2,1)}, bf16[1024,1024]{1,0:T(8,128)(2,1)S(1)}, u32[]{:S(2)}) copy-start(bf16[1024,1024]{1,0:T(8,128)(2,1)S(1)} %multiply_convert_fusion.1) | copy-start | bytes 6291460
  212.1 31.4 %copy-start.2 = (bf16[1024,1024]{1,0:T(8,128)(2,1)}, bf16[1024,1024]{1,0:T(8,128)(2,1)S(1)}, u32[]{:S(2)}) copy-start(bf16[1024,1024]{1,0:T(8,128)(2,1)S(1)} %multiply_convert_fusion.2) | copy-start | bytes 6291460
  230.3 13.6 %copy-start.4 = (bf16[1024,1024]{1,0:T(8,128)(2,1)}, bf16[1024,1024]{1,0:T(8,128)(2,1)S(1)}, u32[]{:S(2)}) copy-start(bf16[1024,1024]{1,0:T(8,128)(2,1)S(1)} %multiply_convert_fusion.3) | copy-start | bytes 6291460
  241.9 8.6 %collective-permute-start.3 = (f32[4,128,128]{2,1,0:T(8,128)S(1)}, f32[4,128,128]{2,1,0:T(8,128)S(1)}, u32[]{:S(2)}, u32[]{:S(2)}) collective-permute-start(f32[4,128,128]{2,1,0:T(8,128)S(1)} %copy-done.11), channel_id=1, source_target_pairs={{0,4},{4,0},{8,12},{12,8},{16,20},{20,16},{24,28},{28,24},{1,5},{5... | collective-permute-start | bytes 786440 | tf_op jit(solution)/shard_map/ppermute | solution.py:26
  245.8 19.4 %collective-permute-start.6 = (f32[3,4,128,128]{3,2,1,0:T(8,128)S(1)}, f32[3,4,128,128]{3,2,1,0:T(8,128)S(1)}, u32[]{:S(2)}, u32[]{:S(2)}) collective-permute-start(f32[3,4,128,128]{3,2,1,0:T(8,128)S(1)} %pad_maximum_fusion), channel_id=1, source_target_pairs={{0,4},{4,0},{8,12},{12,8},{16,20},{20,16},{24,28},{28,24},{1,5},{5... | collective-permute-start | bytes 2359304 | tf_op jit(solution)/shard_map/ppermute | solution.py:26
  250.6 17.3 %collective-permute-start.4 = (f32[4,128,128]{2,1,0:T(8,128)S(1)}, f32[4,128,128]{2,1,0:T(8,128)S(1)}, u32[]{:S(2)}, u32[]{:S(2)}) collective-permute-start(f32[4,128,128]{2,1,0:T(8,128)S(1)} %add.962), channel_id=1, source_target_pairs={{0,8},{8,0},{4,12},{12,4},{16,24},{24,16},{20,28},{28,20},{1,9},{9... | collective-permute-start | bytes 786440 | tf_op jit(solution)/shard_map/ppermute | solution.py:26
  265.3 15.2 %collective-permute-start.7 = (f32[2,4,128,128]{3,2,1,0:T(8,128)S(1)}, f32[2,4,128,128]{3,2,1,0:T(8,128)S(1)}, u32[]{:S(2)}, u32[]{:S(2)}) collective-permute-start(f32[2,4,128,128]{3,2,1,0:T(8,128)S(1)} %slice_add_fusion), channel_id=1, source_target_pairs={{0,8},{8,0},{4,12},{12,4},{16,24},{24,16},{20,28},{28,20},{1,9},{9... | collective-permute-start | bytes 1572872 | tf_op jit(solution)/shard_map/ppermute | solution.py:26
  267.9 14.6 %copy-start.9 = (f32[4,128,128]{2,1,0:T(8,128)}, f32[4,128,128]{2,1,0:T(8,128)S(1)}, u32[]{:S(2)}) copy-start(f32[4,128,128]{2,1,0:T(8,128)S(1)} %collective-permute-done.4) | copy-start | bytes 786436
  268.0 13.8 %collective-permute-start.5 = (bf16[4,128,128]{2,1,0:T(8,128)(2,1)S(1)}, bf16[4,128,128]{2,1,0:T(8,128)(2,1)S(1)}, u32[]{:S(2)}, u32[]{:S(2)}) collective-permute-start(bf16[4,128,128]{2,1,0:T(8,128)(2,1)S(1)} %add.964), channel_id=1, source_target_pairs={{0,16},{16,0},{4,20},{20,4},{8,24},{24,8},{12,28},{28,12},{1,17},{... | collective-permute-start | bytes 393224 | tf_op jit(solution)/shard_map/ppermute | solution.py:26
  280.6 13.2 %collective-permute-start.8 = (f32[1,4,128,128]{3,2,1,0:T(8,128)S(1)}, f32[1,4,128,128]{3,2,1,0:T(8,128)S(1)}, u32[]{:S(2)}, u32[]{:S(2)}) collective-permute-start(f32[1,4,128,128]{3,2,1,0:T(8,128)S(1)} %slice_add_fusion.1), channel_id=1, source_target_pairs={{0,16},{16,0},{4,20},{20,4},{8,24},{24,8},{12,28},{28,12},{1,17},{... | collective-permute-start | bytes 786440 | tf_op jit(solution)/shard_map/ppermute | solution.py:26
  (14 other events, 65.3 us)
Sparse Core Ops, SparseCore 0:
  10.1 51.7 all-gather.5
  64.1 47.6 all-gather.7
  113.8 47.6 all-gather.3
  309.1 206.4 reduce-scatter.1
